TPU v7x, 32 devices: a whole 2x2x4 slice. The times are simulated.
32 devices in a mesh: tile: 8 (over z, y), col: 4 (over x, core).
Axes of the slice: x: 2, y: 2, z: 4, core: 2. Of those that a mesh axis runs over, the one named last changes fastest.
Arguments:
- latent: bfloat16 [8, 17, 4, 16, 256], P('tile', None, None, 'col'), may hold values from -20 to 20
- intersections: int32 [8], P('tile'), may hold values from 0 to 4, as said below
- norm_gain_one: float32 [256], replicated, may hold values from 0.5 to 1.5
- norm_shift_one: float32 [256], replicated, may hold values from -3 to 3
- weight_one: bfloat16 [3, 3, 3, 256, 256], P(None, None, None, 'col'), may hold values from -0.078125 to 0.078125
- norm_gain_two: float32 [256], replicated, may hold values from 0.5 to 1.5
- norm_shift_two: float32 [256], replicated, may hold values from -3 to 3
- weight_two: bfloat16 [3, 3, 3, 256, 256], P(None, None, None, 'col'), may hold values from -0.078125 to 0.078125
- conv_bias: float32 [256], replicated, may hold values from -1.8 to 1.8
Outputs:
- blended: bfloat16 [8, 17, 4, 16, 256], P('tile', None, None, 'col')
Inputs may be any that keep to these rules, and one draw needn't show every extreme that they name: intersections[0] is 0 and every other entry is 1 to 4; some entry equals 4.
All inputs are finite; a program needn't handle non-finite values.
Results may differ from a plain program's by a relative error of at most 0.0055.
Values may be sent and summed in bfloat16 or wider, within the bound.
A program may use at most 64 MiB of HBM per device.

v0:
```python
import jax
import jax.numpy as jnp
from jax import lax
from jax.sharding import PartitionSpec as P

GROUPS = 32
OVMAX = 4


epsilon = 1e-06


def extended_2(array, sides, width):
    for axis, dim in sides:
        size, length = (lax.axis_size(axis), array.shape[dim])
        up = [(i, (i + 1) % size) for i in range(size - 1)]
        down = [(j, i) for i, j in up]
        last = lax.slice_in_dim(array, length - width, length, axis=dim)
        first = lax.slice_in_dim(array, 0, width, axis=dim)
        before = lax.ppermute(last, axis, up)
        after = lax.ppermute(first, axis, down)
        array = jnp.concatenate([before, array, after], axis=dim)
    return array


def shifted(block, axis, distance):
    devices = range(lax.axis_size(axis))
    route = [(i - distance, i) for i in devices if i - distance in devices]
    return lax.ppermute(block, axis, route)


def conv_taps(padded, kernel):
    frames = padded.shape[0]
    height = padded.shape[1]
    out_width = padded.shape[2] - 2
    channels = padded.shape[3]
    outputs = kernel.shape[4]
    padded = jnp.pad(padded, ((2, 0), (1, 1), (0, 0), (0, 0)))
    running = jnp.zeros((frames * height * out_width, outputs), jnp.float32)
    for tap_t in range(3):
        for tap_h in range(3):
            for tap_w in range(3):
                window = padded[
                    tap_t : tap_t + frames, tap_h : tap_h + height, tap_w : tap_w + out_width
                ]
                running = running + jnp.dot(
                    window.reshape(-1, channels),
                    kernel[tap_t, tap_h, tap_w],
                    preferred_element_type=jnp.float32,
                )
    return running.reshape(frames, height, out_width, outputs)


def conv_layer(padded, weight_shard):
    return conv_taps(padded, lax.all_gather(weight_shard, "col", axis=3, tiled=True))


def group_total(values, per_group):
    return jnp.sum(values, axis=(0, 1, 2)).reshape(GROUPS, per_group).sum(axis=1)


def norm_silu(values, inner, gain, shift):
    channels = values.shape[3]
    per_group = channels // GROUPS
    members = inner.shape[0] * inner.shape[1] * inner.shape[2] * lax.axis_size("col") * per_group
    chan_sums = group_total(inner, per_group)
    group_mean = lax.psum(chan_sums, "col") / members
    centred = inner - jnp.repeat(group_mean, per_group)
    spread = lax.psum(group_total(centred * centred, per_group), "col") / members
    inv_std = lax.rsqrt(spread + epsilon)
    normed = (values - jnp.repeat(group_mean, per_group)) * jnp.repeat(
        inv_std, per_group
    ) * gain + shift
    return jax.nn.silu(normed).astype(jnp.bfloat16)


def shards(
    latent,
    intersections,
    norm_gain_one,
    norm_shift_one,
    weight_one,
    norm_gain_two,
    norm_shift_two,
    weight_two,
    conv_bias,
):
    source = latent[0]
    latent_full = source.astype(jnp.float32)
    act_one = norm_silu(latent_full, latent_full, norm_gain_one, norm_shift_one)
    margin = extended_2(act_one, (("col", 2),), 2)
    hidden = conv_layer(margin, weight_shard=weight_one).astype(jnp.bfloat16)
    hidden_full = hidden.astype(jnp.float32)
    act_two = norm_silu(hidden_full, hidden_full[:, :, 1:-1], norm_gain_two, norm_shift_two)
    own_width = source.shape[2]
    position = lax.axis_index("col") * own_width - 1 + jnp.arange(own_width + 2, dtype=jnp.int32)
    inside = (position >= 0) & (position < own_width * lax.axis_size("col"))
    act_two = jnp.where(inside[None, None, :, None], act_two, jnp.zeros_like(act_two))
    branch = conv_layer(act_two, weight_shard=weight_two)
    decoded = (latent_full + (branch + conv_bias)).astype(jnp.bfloat16)
    frames = decoded.shape[0]
    received = shifted(decoded[frames - OVMAX :], "tile", 1)
    shared = intersections[0]
    extended = jnp.concatenate([received, jnp.zeros_like(received)], axis=0)
    aligned = lax.dynamic_slice_in_dim(extended, OVMAX - shared, OVMAX, 0)
    position_t = jnp.arange(OVMAX, dtype=jnp.int32)
    own_share = ((position_t + 1).astype(jnp.float32) / (shared + 1).astype(jnp.float32))[
        :, None, None, None
    ]
    head = decoded[:OVMAX].astype(jnp.float32)
    active = (position_t < shared)[:, None, None, None]
    mixed = jnp.where(
        active, own_share * head + (1.0 - own_share) * aligned.astype(jnp.float32), head
    )
    blended = jnp.concatenate([mixed.astype(jnp.bfloat16), decoded[OVMAX:]], axis=0)
    return blended[None]


def solution(mesh):
    in_specs = (
        P("tile", None, None, "col", None),
        P("tile"),
        P(),
        P(),
        P(None, None, None, "col", None),
        P(),
        P(),
        P(None, None, None, "col", None),
        P(),
    )
    out_specs = P("tile", None, None, "col", None)
    return jax.shard_map(shards, mesh=mesh, in_specs=in_specs, out_specs=out_specs, check_vma=False)
```

profile of v0, /device:TPU:0, one launch (start us, length us, event | category | flops | bytes accessed | tf_op | source)
XLA Modules:
  0.0 122.0 jit_solution(5098323203788432330)
XLA Ops:
  6.5 0.7 all-gather.3.cloned.1.call-update
  7.3 1.0 convert_reduce_fusion
  8.5 8.4 %psum.28 = f32[32]{0:T(128)S(1)} all-reduce(f32[32]{0:T(128)S(1)} %reduce_sum.73), channel_id=1, replica_groups=mesh['tile'=8,'col'=4] {'col'}, use_global_device_ids=true, to_apply=%region_2.0 | all-reduce | flops 32 | bytes 256 | tf_op jit(solution)/shard_map/psum | solution.py:67
  17.1 1.1 fusion.8
  18.3 6.3 %psum.29 = f32[32]{0:T(128)S(1)} all-reduce(f32[32]{0:T(128)S(1)} %reduce_sum.75), channel_id=1, replica_groups=mesh['tile'=8,'col'=4] {'col'}, use_global_device_ids=true, to_apply=%region_5.0 | all-reduce | flops 32 | bytes 256 | tf_op jit(solution)/shard_map/psum | solution.py:69
  24.8 1.1 fusion.12
  26.0 1.3 %collective-permute-start = (bf16[17,4,2,256]{3,2,1,0:T(2,128)(2,1)S(1)}, bf16[17,4,2,256]{3,2,1,0:T(2,128)(2,1)S(1)}, u32[]{:S(2)}, u32[]{:S(2)}) collective-permute-start(bf16[17,4,2,256]{3,2,1,0:T(2,128)(2,1)S(1)} %get-tuple-element.59), channel_id=1, source_target_pairs={{0,1},{1,2},{2,3},{4,5},{5,6},{6,7},{8,9},{9,10},{10,11},{12,13},{... | collective-permute-start | bytes 208904 | tf_op jit(solution)/shard_map/ppermute | solution.py:20
  27.3 1.3 %collective-permute-start.1 = (bf16[17,4,2,256]{3,2,1,0:T(2,128)(2,1)S(1)}, bf16[17,4,2,256]{3,2,1,0:T(2,128)(2,1)S(1)}, u32[]{:S(2)}, u32[]{:S(2)}) collective-permute-start(bf16[17,4,2,256]{3,2,1,0:T(2,128)(2,1)S(1)} %get-tuple-element.60), channel_id=1, source_target_pairs={{1,0},{2,1},{3,2},{5,4},{6,5},{7,6},{9,8},{10,9},{11,10},{13,12},{... | collective-permute-start | bytes 208904 | tf_op jit(solution)/shard_map/ppermute | solution.py:21
  31.5 2.0 %pad_slice_fusion.24 = (bf16[17,4,6,256]{3,2,1,0:T(8,128)(2,1)S(1)}, bf16[17,4,6,256]{3,2,1,0:T(8,128)(2,1)}, bf16[17,4,6,256]{3,2,1,0:T(8,128)(2,1)}, bf16[17,4...) fusion(bf16[17,4,8,256]{3,2,1,0:T(8,128)(2,1)S(1)} %pad_maximum, ...), kind=kLoop, calls=%fused_computation.24 | loop fusion | bytes 4247552 | tf_op jit(solution)/shard_map/slice | solution.py:43
  33.8 1.7 %reshape.215 = bf16[408,256]{1,0:T(8,128)(2,1)} reshape(bf16[17,4,6,256]{3,2,1,0:T(8,128)(2,1)} %get-tuple-element.33) | data formatting | bytes 417792 | tf_op jit(solution)/shard_map/reshape | solution.py:47
  35.6 0.8 reshape.214
  36.3 1.8 %reshape.216 = bf16[408,256]{1,0:T(8,128)(2,1)} reshape(bf16[17,4,6,256]{3,2,1,0:T(8,128)(2,1)} %get-tuple-element.34) | data formatting | bytes 417792 | tf_op jit(solution)/shard_map/reshape | solution.py:47
  38.1 1.7 %reshape.217 = bf16[408,256]{1,0:T(8,128)(2,1)} reshape(bf16[17,4,6,256]{3,2,1,0:T(8,128)(2,1)} %get-tuple-element.35) | data formatting | bytes 417792 | tf_op jit(solution)/shard_map/reshape | solution.py:47
  39.8 1.7 %reshape.218 = bf16[408,256]{1,0:T(8,128)(2,1)} reshape(bf16[17,4,6,256]{3,2,1,0:T(8,128)(2,1)} %get-tuple-element.36) | data formatting | bytes 417792 | tf_op jit(solution)/shard_map/reshape | solution.py:47
  41.5 1.7 %reshape.219 = bf16[408,256]{1,0:T(8,128)(2,1)} reshape(bf16[17,4,6,256]{3,2,1,0:T(8,128)(2,1)} %get-tuple-element.37) | data formatting | bytes 417792 | tf_op jit(solution)/shard_map/reshape | solution.py:47
  43.3 1.7 %reshape.220 = bf16[408,256]{1,0:T(8,128)(2,1)} reshape(bf16[17,4,6,256]{3,2,1,0:T(8,128)(2,1)} %get-tuple-element.38) | data formatting | bytes 417792 | tf_op jit(solution)/shard_map/reshape | solution.py:47
  45.0 1.7 %reshape.221 = bf16[408,256]{1,0:T(8,128)(2,1)} reshape(bf16[17,4,6,256]{3,2,1,0:T(8,128)(2,1)} %get-tuple-element.39) | data formatting | bytes 417792 | tf_op jit(solution)/shard_map/reshape | solution.py:47
  46.7 1.7 %reshape.222 = bf16[408,256]{1,0:T(8,128)(2,1)} reshape(bf16[17,4,6,256]{3,2,1,0:T(8,128)(2,1)} %get-tuple-element.40) | data formatting | bytes 417792 | tf_op jit(solution)/shard_map/reshape | solution.py:47
  48.4 1.7 %reshape.223 = bf16[408,256]{1,0:T(8,128)(2,1)} reshape(bf16[17,4,6,256]{3,2,1,0:T(8,128)(2,1)} %get-tuple-element.41) | data formatting | bytes 417792 | tf_op jit(solution)/shard_map/reshape | solution.py:47
  50.1 1.8 %reshape.224 = bf16[408,256]{1,0:T(8,128)(2,1)} reshape(bf16[17,4,6,256]{3,2,1,0:T(8,128)(2,1)} %get-tuple-element.42) | data formatting | bytes 417792 | tf_op jit(solution)/shard_map/reshape | solution.py:47
  51.9 1.7 %reshape.225 = bf16[408,256]{1,0:T(8,128)(2,1)} reshape(bf16[17,4,6,256]{3,2,1,0:T(8,128)(2,1)} %get-tuple-element.43) | data formatting | bytes 417792 | tf_op jit(solution)/shard_map/reshape | solution.py:47
  53.7 1.7 %reshape.226 = bf16[408,256]{1,0:T(8,128)(2,1)} reshape(bf16[17,4,6,256]{3,2,1,0:T(8,128)(2,1)} %get-tuple-element.44) | data formatting | bytes 417792 | tf_op jit(solution)/shard_map/reshape | solution.py:47
  55.4 0.8 reshape.227
  56.7 0.7 reshape.236
  57.7 0.8 reshape.235
  58.5 0.7 reshape.238
  59.2 0.7 reshape.237
  60.2 1.4 %fusion.17 = f32[408,256]{1,0:T(8,128)S(1)} fusion(bf16[408,256]{1,0:T(8,128)(2,1)} %reshape.215, bf16[3,3,3,256,256]{4,3,2,1,0:T(8,128)(2,1)} %all-gather.3.cloned.1.call-done), kind=kOutput, calls=%fused_computation.178 | convolution fusion | flops 53477376 | bytes 757760 | tf_op jit(solution)/shard_map/dot_general | solution.py:46
  61.6 1.2 fusion.16
  62.8 1.3 %convolution_add_fusion.23 = f32[408,256]{1,0:T(8,128)S(1)} fusion(f32[408,256]{1,0:T(8,128)S(1)} %fusion.17, bf16[408,256]{1,0:T(8,128)(2,1)} %reshape.214, bf16[3,3,3,256,256]{4,3,2,1,0:T(8,128)(2,1)} %all-gather.3.cloned.1.call-done), kind=kOutput, calls=%fused_computation.71 | convolution fusion | flops 53581824 | bytes 1175552 | tf_op jit(solution)/shard_map/dot_general | solution.py:46
  64.1 1.3 %convolution_add_fusion.22 = f32[408,256]{1,0:T(8,128)S(1)} fusion(f32[408,256]{1,0:T(8,128)S(1)} %convolution_add_fusion.23, bf16[408,256]{1,0:T(8,128)(2,1)} %reshape.216, bf16[3,3,3,256,256]{4,3,2,1,0:T(8,128)(2,1)} %all-gather.3.cloned.1.call-done), kind=kOutput, calls=%fused_computation.70 | convolution fusion | flops 53581824 | bytes 1175552 | tf_op jit(solution)/shard_map/dot_general | solution.py:46
  65.4 1.2 convolution_add_fusion.21
  66.6 1.2 convolution_add_fusion.20
  73.2 10.6 %psum.30 = f32[32]{0:T(128)S(1)} all-reduce(f32[32]{0:T(128)S(1)} %reduce_sum.77), channel_id=1, replica_groups=mesh['tile'=8,'col'=4] {'col'}, use_global_device_ids=true, to_apply=%region_8.9 | all-reduce | flops 32 | bytes 256 | tf_op jit(solution)/shard_map/psum | solution.py:67
  84.4 5.8 %psum.31 = f32[32]{0:T(128)S(1)} all-reduce(f32[32]{0:T(128)S(1)} %reduce_sum.79), channel_id=1, replica_groups=mesh['tile'=8,'col'=4] {'col'}, use_global_device_ids=true, to_apply=%region_11.12 | all-reduce | flops 32 | bytes 256 | tf_op jit(solution)/shard_map/psum | solution.py:69
  90.6 0.8 pad_slice_fusion
  91.5 1.2 pad_slice_fusion.1
  95.4 0.9 reshape.262
  96.3 0.9 reshape.263
  97.4 0.9 reshape.266
  98.5 1.3 %fusion.14 = f32[272,256]{1,0:T(8,128)S(1)} fusion(bf16[272,256]{1,0:T(8,128)(2,1)} %reshape.243, bf16[3,3,3,256,256]{4,3,2,1,0:T(8,128)(2,1)} %all-gather.5.cloned.1.call-done), kind=kOutput, calls=%fused_computation.149 | convolution fusion | flops 35651584 | bytes 548864 | tf_op jit(solution)/shard_map/dot_general | solution.py:46
  99.8 1.1 convolution_add_fusion.49
  100.9 1.2 convolution_add_fusion.48
  102.1 1.2 convolution_add_fusion.47
  103.3 1.1 convolution_add_fusion.46
  109.0 3.6 %collective-permute-start.2 = (bf16[4,4,4,256]{3,2,1,0:T(4,128)(2,1)S(1)}, bf16[4,4,4,256]{3,2,1,0:T(4,128)(2,1)S(1)}, u32[]{:S(2)}, u32[]{:S(2)}) collective-permute-start(bf16[4,4,4,256]{3,2,1,0:T(4,128)(2,1)S(1)} %slice.520), channel_id=1, source_target_pairs={{0,4},{4,8},{8,12},{12,16},{16,20},{20,24},{24,28},{1,5},{5,9},{9,... | collective-permute-start | bytes 98312 | tf_op jit(solution)/shard_map/ppermute | solution.py:29
  112.7 1.5 %collective-permute-done.2 = bf16[4,4,4,256]{3,2,1,0:T(4,128)(2,1)S(1)} collective-permute-done((bf16[4,4,4,256]{3,2,1,0:T(4,128)(2,1)S(1)}, bf16[4,4,4,256]{3,2,1,0:T(4,128)(2,1)S(1)}, u32[]{:S(2)}, u32[]{:S(2)}) %collective-permute-start.2) | collective-permute-done | bytes 32800 | tf_op jit(solution)/shard_map/ppermute | solution.py:29
  114.4 0.8 maximum_bitcast_fusion
  (169 shorter events, 17.9 us)
Async XLA Ops:
  6.5 53.6 %all-gather.3.cloned.1.call-start = ((), (), s32[]{:S(2)}) async-start(), calls=%async_computation | async-start | bytes 4423680 | tf_op jit(solution)/shard_map/all_gather | solution.py:55
  7.3 91.2 %all-gather.5.cloned.1.call-start = ((), (), s32[]{:S(2)}) async-start(), calls=%async_computation.1 | async-start | bytes 4423680 | tf_op jit(solution)/shard_map/all_gather | solution.py:55
  26.0 4.3 %collective-permute-start = (bf16[17,4,2,256]{3,2,1,0:T(2,128)(2,1)S(1)}, bf16[17,4,2,256]{3,2,1,0:T(2,128)(2,1)S(1)}, u32[]{:S(2)}, u32[]{:S(2)}) collective-permute-start(bf16[17,4,2,256]{3,2,1,0:T(2,128)(2,1)S(1)} %get-tuple-element.59), channel_id=1, source_target_pairs={{0,1},{1,2},{2,3},{4,5},{5,6},{6,7},{8,9},{9,10},{10,11},{12,13},{... | collective-permute-start | bytes 208904 | tf_op jit(solution)/shard_map/ppermute | solution.py:20
  27.3 3.3 %collective-permute-start.1 = (bf16[17,4,2,256]{3,2,1,0:T(2,128)(2,1)S(1)}, bf16[17,4,2,256]{3,2,1,0:T(2,128)(2,1)S(1)}, u32[]{:S(2)}, u32[]{:S(2)}) collective-permute-start(bf16[17,4,2,256]{3,2,1,0:T(2,128)(2,1)S(1)} %get-tuple-element.60), channel_id=1, source_target_pairs={{1,0},{2,1},{3,2},{5,4},{6,5},{7,6},{9,8},{10,9},{11,10},{13,12},{... | collective-permute-start | bytes 208904 | tf_op jit(solution)/shard_map/ppermute | solution.py:21
  30.7 0.6 copy-start.18
  36.3 19.0 %copy-start.3 = (bf16[17,4,6,256]{3,2,1,0:T(8,128)(2,1)S(1)}, bf16[17,4,6,256]{3,2,1,0:T(8,128)(2,1)}, u32[]{:S(2)}) copy-start(bf16[17,4,6,256]{3,2,1,0:T(8,128)(2,1)} %get-tuple-element.45) | copy-start | bytes 626692
  56.1 1.3 %copy-start.19 = (bf16[17,4,2,256]{3,2,1,0:T(2,128)(2,1)S(1)}, bf16[17,4,2,256]{3,2,1,0:T(2,128)(2,1)}, u32[]{:S(2)}) copy-start(bf16[17,4,2,256]{3,2,1,0:T(2,128)(2,1)} %copy-done.18) | copy-start | bytes 208900
  60.1 7.8 %copy-start.14 = (bf16[408,256]{1,0:T(8,128)(2,1)S(1)}, bf16[408,256]{1,0:T(8,128)(2,1)}, u32[]{:S(2)}) copy-start(bf16[408,256]{1,0:T(8,128)(2,1)} %reshape.219) | copy-start | bytes 626692
  60.1 7.9 %copy-start.13 = (bf16[408,256]{1,0:T(8,128)(2,1)S(1)}, bf16[408,256]{1,0:T(8,128)(2,1)}, u32[]{:S(2)}) copy-start(bf16[408,256]{1,0:T(8,128)(2,1)} %reshape.220) | copy-start | bytes 626692
  60.2 5.2 %copy-start.1 = (bf16[3,3,3,256,256]{4,3,2,1,0:T(8,128)(2,1)S(1)}, bf16[3,3,3,256,256]{4,3,2,1,0:T(8,128)(2,1)}, u32[]{:S(2)}) copy-start(bf16[3,3,3,256,256]{4,3,2,1,0:T(8,128)(2,1)} %all-gather.3.cloned.1.call-done) | copy-start | bytes 10616836
  62.8 5.5 %copy-start.12 = (bf16[408,256]{1,0:T(8,128)(2,1)S(1)}, bf16[408,256]{1,0:T(8,128)(2,1)}, u32[]{:S(2)}) copy-start(bf16[408,256]{1,0:T(8,128)(2,1)} %reshape.221) | copy-start | bytes 626692
  64.1 4.4 %copy-start.11 = (bf16[408,256]{1,0:T(8,128)(2,1)S(1)}, bf16[408,256]{1,0:T(8,128)(2,1)}, u32[]{:S(2)}) copy-start(bf16[408,256]{1,0:T(8,128)(2,1)} %reshape.222) | copy-start | bytes 626692
  65.4 3.4 %copy-start.10 = (bf16[408,256]{1,0:T(8,128)(2,1)S(1)}, bf16[408,256]{1,0:T(8,128)(2,1)}, u32[]{:S(2)}) copy-start(bf16[408,256]{1,0:T(8,128)(2,1)} %reshape.223) | copy-start | bytes 626692
  66.6 2.4 %copy-start.15 = (bf16[408,256]{1,0:T(8,128)(2,1)S(1)}, bf16[408,256]{1,0:T(8,128)(2,1)}, u32[]{:S(2)}) copy-start(bf16[408,256]{1,0:T(8,128)(2,1)} %reshape.238) | copy-start | bytes 626692
  67.8 1.5 %copy-start.9 = (bf16[408,256]{1,0:T(8,128)(2,1)S(1)}, bf16[408,256]{1,0:T(8,128)(2,1)}, u32[]{:S(2)}) copy-start(bf16[408,256]{1,0:T(8,128)(2,1)} %reshape.224) | copy-start | bytes 626692
  68.1 1.4 %copy-start.8 = (bf16[408,256]{1,0:T(8,128)(2,1)S(1)}, bf16[408,256]{1,0:T(8,128)(2,1)}, u32[]{:S(2)}) copy-start(bf16[408,256]{1,0:T(8,128)(2,1)} %reshape.225) | copy-start | bytes 626692
  68.3 1.4 %copy-start.6 = (bf16[408,256]{1,0:T(8,128)(2,1)S(1)}, bf16[408,256]{1,0:T(8,128)(2,1)}, u32[]{:S(2)}) copy-start(bf16[408,256]{1,0:T(8,128)(2,1)} %reshape.226) | copy-start | bytes 626692
  68.6 1.4 %copy-start.4 = (bf16[408,256]{1,0:T(8,128)(2,1)S(1)}, bf16[408,256]{1,0:T(8,128)(2,1)}, u32[]{:S(2)}) copy-start(bf16[408,256]{1,0:T(8,128)(2,1)} %reshape.227) | copy-start | bytes 626692
  70.5 1.4 %copy-start.5 = (bf16[408,256]{1,0:T(8,128)(2,1)S(1)}, bf16[408,256]{1,0:T(8,128)(2,1)}, u32[]{:S(2)}) copy-start(bf16[408,256]{1,0:T(8,128)(2,1)} %reshape.235) | copy-start | bytes 626692
  70.7 1.4 %copy-start.7 = (bf16[408,256]{1,0:T(8,128)(2,1)S(1)}, bf16[408,256]{1,0:T(8,128)(2,1)}, u32[]{:S(2)}) copy-start(bf16[408,256]{1,0:T(8,128)(2,1)} %reshape.237) | copy-start | bytes 626692
  71.9 18.5 %copy-start.20 = (f32[256]{0:T(256)S(1)}, f32[256]{0:T(256)}, u32[]{:S(2)}) copy-start(f32[256]{0:T(256)} %param.15) | copy-start | bytes 3076
  71.9 18.5 %copy-start.21 = (f32[256]{0:T(256)S(1)}, f32[256]{0:T(256)}, u32[]{:S(2)}) copy-start(f32[256]{0:T(256)} %param.14) | copy-start | bytes 3076
  71.9 18.5 %copy-start.24 = (pred[6]{0:T(512)(128)(4,1)S(1)}, pred[6]{0:T(512)(128)(4,1)}, u32[]{:S(2)}) copy-start(pred[6]{0:T(512)(128)(4,1)} %compare_and_fusion) | copy-start | bytes 22
  92.7 4.6 %copy-start.17 = (bf16[17,4,4,256]{3,2,1,0:T(4,128)(2,1)S(1)}, bf16[17,4,4,256]{3,2,1,0:T(4,128)(2,1)}, u32[]{:S(2)}) copy-start(bf16[17,4,4,256]{3,2,1,0:T(4,128)(2,1)} %get-tuple-element.30) | copy-start | bytes 417796
  92.7 4.6 %copy-start.16 = (bf16[17,4,4,256]{3,2,1,0:T(4,128)(2,1)S(1)}, bf16[17,4,4,256]{3,2,1,0:T(4,128)(2,1)}, u32[]{:S(2)}) copy-start(bf16[17,4,4,256]{3,2,1,0:T(4,128)(2,1)} %get-tuple-element.29) | copy-start | bytes 417796
  98.5 5.9 %copy-start = (bf16[3,3,3,256,256]{4,3,2,1,0:T(8,128)(2,1)S(1)}, bf16[3,3,3,256,256]{4,3,2,1,0:T(8,128)(2,1)}, u32[]{:S(2)}) copy-start(bf16[3,3,3,256,256]{4,3,2,1,0:T(8,128)(2,1)} %all-gather.5.cloned.1.call-done) | copy-start | bytes 10616836
  107.2 1.7 %copy-start.2 = (bf16[1,17,4,4,256]{4,3,2,1,0:T(4,128)(2,1)S(1)}, bf16[1,17,4,4,256]{4,3,2,1,0:T(4,128)(2,1)}, u32[]{:S(2)}) copy-start(bf16[1,17,4,4,256]{4,3,2,1,0:T(4,128)(2,1)} %param.9) | copy-start | bytes 417796
  107.2 1.7 %copy-start.22 = (f32[256]{0:T(256)S(1)}, f32[256]{0:T(256)}, u32[]{:S(2)}) copy-start(f32[256]{0:T(256)} %param.17) | copy-start | bytes 3076
  107.4 6.8 %copy-start.23 = (f32[4]{0:T(128)S(1)}, f32[4]{0:T(128)}, u32[]{:S(2)}) copy-start(f32[4]{0:T(128)} %get-tuple-element.62) | copy-start | bytes 52
  109.0 5.2 %collective-permute-start.2 = (bf16[4,4,4,256]{3,2,1,0:T(4,128)(2,1)S(1)}, bf16[4,4,4,256]{3,2,1,0:T(4,128)(2,1)S(1)}, u32[]{:S(2)}, u32[]{:S(2)}) collective-permute-start(bf16[4,4,4,256]{3,2,1,0:T(4,128)(2,1)S(1)} %slice.520), channel_id=1, source_target_pairs={{0,4},{4,8},{8,12},{12,16},{16,20},{20,24},{24,28},{1,5},{5,9},{9,... | collective-permute-start | bytes 98312 | tf_op jit(solution)/shard_map/ppermute | solution.py:29
Sparse Core Ops, SparseCore 0:
  8.9 34.3 all-gather.2
  44.8 30.7 all-gather.4
where the time goes:
time: 123 us; the launch traced here: 122 us
  local copies, waits for them, and re-layouts  38 us (31%)
  blocking collectives  31.1 us (25%)
  matrix products  22.3 us (18%)
  between operations  15.1 us (12%)
  other arithmetic  6.67 us (5%)
  starting transfers between devices  6.25 us (5%)
  waiting for transfers between devices  2.6 us (2%)
    reshape x54, local copies, waits for them, and re-layouts, conv_taps(): window.reshape(-1, channels)  31.7 us
    dot_general x54, matrix products, conv_taps(): jnp.dot(window.reshape(-1, channels), kernel[tap_t, tap_h, tap_w], prefer...  22.3 us
    psum x2, blocking collectives, norm_silu(): group_mean = lax.psum(chan_sums, 'col') / members  19 us
    psum x2, blocking collectives, norm_silu(): lax.psum(group_total(centred * centred, per_group), 'col') / members  12.1 us
    slice x4, local copies, waits for them, and re-layouts, conv_taps(): padded[tap_t:tap_t + frames, tap_h:tap_h + height, tap_w:tap_w + out_width]  4.31 us
    ppermute x1, starting transfers between devices, shifted(): return lax.ppermute(block, axis, route)  3.63 us
    reduce_sum x8, other arithmetic, group_total(): jnp.sum(values, axis=(0, 1, 2)).reshape(GROUPS, per_group).sum(axis=1)  2.8 us
  transfers between devices with their start and end apart: 5, of which 2 were waited for; matrix products, arithmetic and copies ran while one was open for 45% of the time, Pallas kernels for 0%

commit v1 on v0

--- a/solution.py
+++ b/solution.py
@@ -1,6 +1,10 @@
+import functools
+
 import jax
 import jax.numpy as jnp
 from jax import lax
+from jax.experimental import pallas as pl
+from jax.experimental.pallas import tpu as pltpu
 from jax.sharding import PartitionSpec as P
 
 GROUPS = 32
@@ -116,6 +120,391 @@
     return blended[None]
 
 
+MESH = pl.DeviceIdType.MESH
+LANES = 128
+
+
+def group_sum(row, per_group):
+    lane = lax.broadcasted_iota(jnp.int32, row.shape, 1)
+    width = row.shape[1]
+    step = 1
+    while step < per_group:
+        up = pltpu.roll(row, width - step, 1)
+        down = pltpu.roll(row, step, 1)
+        row = row + jnp.where((lane & step) == 0, up, down)
+        step *= 2
+    return row
+
+
+def norm_into(lines, taps, gain, shift, per_group):
+    frames = taps.shape[0] - 2
+    height, width = taps.shape[1] - 2, taps.shape[2]
+    members = frames * height * width * per_group
+
+    def total(f):
+        acc = jnp.zeros((8, LANES), jnp.float32)
+        for t in range(frames):
+            acc = acc + f(lines(t)).reshape(-1, 8, LANES).sum(axis=0)
+        row = jnp.broadcast_to(acc.sum(axis=0, keepdims=True), (8, LANES))
+        return group_sum(row, per_group)[0:1] / members
+
+    mean = total(lambda v: v)
+
+    def square(v):
+        d = v - mean[None]
+        return d * d
+
+    scale = lax.rsqrt(total(square) + epsilon)
+    where = lax.broadcasted_iota(jnp.int32, (height, width, LANES), 1)
+    for t in range(frames):
+        v = (lines(t) - mean[None]) * scale[None] * gain[None] + shift[None]
+        a = v / (1.0 + jnp.exp(-v))
+        left = jnp.where(where == 0, 0.0, pltpu.roll(a, 1, 1))
+        right = jnp.where(where == width - 1, 0.0, pltpu.roll(a, width - 1, 1))
+        place = (t + 2, pl.ds(1, height))
+        taps[place + (slice(None), pl.ds(0, LANES))] = left.astype(jnp.bfloat16)
+        taps[place + (slice(None), pl.ds(LANES, LANES))] = a.astype(jnp.bfloat16)
+        taps[place + (slice(None), pl.ds(2 * LANES, LANES))] = right.astype(jnp.bfloat16)
+
+
+def conv_part(taps, weight, first, count, row, rows):
+    width, depth = taps.shape[2], taps.shape[3]
+    pieces = []
+    for dt in range(3):
+        for dh in range(3):
+            window = taps[pl.ds(first + dt, count), pl.ds(row + dh, rows)]
+            pieces.append(window.reshape(count * rows * width, depth))
+    lhs = jnp.concatenate(pieces, axis=1)
+    rhs = weight[...].reshape(9 * depth, weight.shape[2])
+    return jnp.dot(lhs, rhs, preferred_element_type=jnp.float32)
+
+
+def block_kernel(
+    tiles,
+    chunks_one,
+    chunks_two,
+    inter,
+    lat,
+    gain_one,
+    shift_one,
+    gain_two,
+    shift_two,
+    bias,
+    w_one,
+    w_two,
+    out,
+    wb_one,
+    wb_two,
+    got,
+    full,
+    taps,
+    part_out,
+    part_in,
+    keep_one,
+    hid,
+    mix_out,
+    mix_in,
+    keep_two,
+    give,
+    take,
+    tail_in,
+    w_local,
+    w_send,
+    w_recv,
+    l_send,
+    l_recv,
+    p_send,
+    p_recv,
+    h_send,
+    h_recv,
+    m_send,
+    m_recv,
+    g_send,
+    g_recv,
+    t_send,
+    t_recv,
+):
+    tile = lax.axis_index("tile")
+    me = lax.axis_index("col")
+    chip = me // 2
+    core = me % 2
+    partner = chip * 2 + (1 - core)
+    twin = (1 - chip) * 2 + core
+    frames, height, own_width, channels = lat.shape
+    shard = channels // 4
+    half = channels // 2
+    rows = height // 2
+    width = 4 * own_width
+
+    def remote(src, dst, send, recv, col):
+        return pltpu.make_async_remote_copy(
+            src_ref=src,
+            dst_ref=dst,
+            send_sem=send,
+            recv_sem=recv,
+            device_id={"tile": tile, "col": col},
+            device_id_type=MESH,
+        )
+
+    mine_rows = pl.ds(pl.multiple_of(core * shard, shard), shard)
+    w_copies = []
+    for k, (w, wb) in enumerate(((w_one, wb_one), (w_two, wb_two))):
+        copy = pltpu.make_async_copy(w, wb.at[:, mine_rows, :], w_local.at[k])
+        copy.start()
+        w_copies.append(copy)
+
+    barrier = pltpu.get_barrier_semaphore()
+    for col in (partner, twin):
+        pl.semaphore_signal(
+            barrier, inc=1, device_id={"tile": tile, "col": col}, device_id_type=MESH
+        )
+
+    @pl.when(tile > 0)
+    def _():
+        pl.semaphore_signal(
+            barrier, inc=1, device_id={"tile": tile - 1, "col": me}, device_id_type=MESH
+        )
+
+    @pl.when(tile < tiles - 1)
+    def _():
+        pl.semaphore_signal(
+            barrier, inc=1, device_id={"tile": tile + 1, "col": me}, device_id_type=MESH
+        )
+
+    pl.semaphore_wait(
+        barrier, 2 + jnp.where(tile > 0, 1, 0) + jnp.where(tile < tiles - 1, 1, 0)
+    )
+
+    here = pl.ds(pl.multiple_of(chip * half, half), half)
+    there = pl.ds(pl.multiple_of((1 - chip) * half, half), half)
+    to_twin = remote(lat.at[:, :, :, there], got.at[me], l_send.at[0], l_recv.at[0], twin)
+    to_twin.start()
+    to_partner = remote(lat.at[:, :, :, here], got.at[me], l_send.at[1], l_recv.at[1], partner)
+    to_partner.start()
+    w_sends = []
+    for k, (w, wb) in enumerate(((w_one, wb_one), (w_two, wb_two))):
+        copy = remote(w, wb.at[:, mine_rows, :], w_send.at[k], w_recv.at[k], partner)
+        copy.start()
+        w_sends.append(copy)
+
+    taps[0:2] = jnp.zeros((2,) + taps.shape[1:], taps.dtype)
+    edge = jnp.zeros((frames,) + taps.shape[2:], taps.dtype)
+    taps[2:, 0] = edge
+    taps[2:, height + 1] = edge
+
+    first_chip = chip == 0
+    first_core = core == 0
+
+    def chosen(ref):
+        return jnp.where(first_chip, ref[:, :half], ref[:, half:])
+
+    got[me] = jnp.where(first_chip, lat[:, :, :, :half], lat[:, :, :, half:])
+
+    to_twin.wait_recv()
+    forward = remote(got.at[twin], got.at[twin], l_send.at[2], l_recv.at[2], partner)
+    forward.start()
+    to_partner.wait_recv()
+    forward.wait_recv()
+    for i in range(4):
+        full[:, :, i * own_width : (i + 1) * own_width, :] = got[i].astype(jnp.float32)
+
+    per_group = channels // GROUPS
+    norm_into(
+        lambda t: full[t], taps, chosen(gain_one), chosen(shift_one), per_group
+    )
+
+    w_copies[0].wait()
+    w_sends[0].wait()
+    row = core * rows
+    sends = []
+    start = 0
+    for k, count in enumerate(chunks_one):
+        acc = conv_part(taps, wb_one, start, count, row, rows)
+        lo, hi = acc[:, :half], acc[:, half:]
+        span = pl.ds(start * rows * width, count * rows * width)
+        part_out[span] = jnp.where(first_chip, hi, lo).astype(jnp.bfloat16)
+        copy = remote(part_out.at[span], part_in.at[span], p_send.at[k], p_recv.at[k], twin)
+        copy.start()
+        keep_one[span] = jnp.where(first_chip, lo, hi)
+        sends.append((copy, span, start, count))
+        start += count
+    back = []
+    for k, (copy, span, first, count) in enumerate(sends):
+        copy.wait_recv()
+        value = keep_one[span] + part_in[span].astype(jnp.float32)
+        place = (pl.ds(first, count), pl.ds(row, rows))
+        hid[place] = value.astype(jnp.bfloat16).reshape(count, rows, width, half)
+        copy = remote(hid.at[place], hid.at[place], h_send.at[k], h_recv.at[k], partner)
+        copy.start()
+        back.append(copy)
+    for copy in back:
+        copy.wait_recv()
+
+    norm_into(
+        lambda t: hid[t].astype(jnp.float32), taps, chosen(gain_two), chosen(shift_two), per_group
+    )
+
+    w_copies[1].wait()
+    w_sends[1].wait()
+    cols = 2 * own_width
+    sends_two = []
+    for k, (first, count) in enumerate(chunks_two):
+        acc = conv_part(taps, wb_two, first, count, row, rows)
+        acc = acc.reshape(count * rows, width, channels)
+        lo, hi = acc[:, :cols], acc[:, cols:]
+        span = pl.ds(first * rows * cols, count * rows * cols)
+        away = jnp.where(first_chip, hi, lo).reshape(count * rows * cols, channels)
+        mix_out[span] = away.astype(jnp.bfloat16)
+        copy = remote(mix_out.at[span], mix_in.at[span], m_send.at[k], m_recv.at[k], twin)
+        copy.start()
+        keep_two[span] = jnp.where(first_chip, lo, hi).reshape(count * rows * cols, channels)
+        sends_two.append((copy, span, first, count))
+
+    other_row = (1 - core) * rows
+    offset = bias[...][None, None]
+
+    def finish(place, values):
+        own = lat[place].astype(jnp.float32)
+        out[place] = (own + (values + offset)).astype(jnp.bfloat16)
+
+    overlap = OVMAX
+    next_tile = jnp.minimum(tile + 1, tiles - 1)
+    tail_copy = pltpu.make_async_remote_copy(
+        src_ref=out.at[pl.ds(frames - overlap, overlap)],
+        dst_ref=tail_in,
+        send_sem=t_send,
+        recv_sem=t_recv,
+        device_id={"tile": next_tile, "col": me},
+        device_id_type=MESH,
+    )
+    gives = []
+    for k, (copy, span, first, count) in enumerate(sends_two):
+        copy.wait_recv()
+        value = keep_two[span] + mix_in[span].astype(jnp.float32)
+        value = value.reshape(count * rows, cols, channels)
+        lo, hi = value[:, :own_width], value[:, own_width:]
+        times = pl.ds(first, count)
+        theirs = jnp.where(first_core, hi, lo)
+        give[times] = theirs.reshape(count, rows, own_width, channels)
+        swap = remote(give.at[times], take.at[times], g_send.at[k], g_recv.at[k], partner)
+        swap.start()
+        gives.append(swap)
+        ours = jnp.where(first_core, lo, hi).reshape(count, rows, own_width, channels)
+        finish((times, pl.ds(row, rows)), ours)
+        swap.wait_recv()
+        finish((times, pl.ds(other_row, rows)), take[times])
+        if k == 0:
+
+            @pl.when(tile < tiles - 1)
+            def _():
+                tail_copy.start()
+
+    @pl.when(tile > 0)
+    def _():
+        tail_copy.wait_recv()
+
+    @pl.when(tile == 0)
+    def _():
+        tail_in[...] = jnp.zeros(tail_in.shape, tail_in.dtype)
+
+    shared = inter[0]
+    whole = jnp.full((height, own_width, channels), shared + 1, jnp.int32).astype(jnp.float32)
+    for j in range(overlap):
+        u = (j + 1) / whole
+        before = tail_in[jnp.clip(overlap - shared + j, 0, overlap - 1)].astype(jnp.float32)
+        value = out[j].astype(jnp.float32)
+        mixed = jnp.where(j < shared, u * value + (1.0 - u) * before, value)
+        out[j] = mixed.astype(jnp.bfloat16)
+
+    to_twin.wait_send()
+    to_partner.wait_send()
+    forward.wait_send()
+    for copy, _, _, _ in sends + sends_two:
+        copy.wait_send()
+    for copy in back + gives:
+        copy.wait_send()
+
+    @pl.when(tile < tiles - 1)
+    def _():
+        tail_copy.wait_send()
+
+
+def fused(tiles, latent, intersections, gain_one, shift_one, weight_one, gain_two, shift_two, weight_two, bias):
+    _, frames, height, own_width, channels = latent.shape
+    width, half, rows = 4 * own_width, channels // 2, height // 2
+    ahead = (frames + 1) // 2
+    chunks_one = (ahead, frames - ahead)
+    chunks_two = ((frames - OVMAX, OVMAX), (0, frames - OVMAX))
+    shard = weight_one.shape[3]
+    vmem = pl.BlockSpec(memory_space=pltpu.VMEM)
+    anywhere = pl.BlockSpec(memory_space=pl.ANY)
+    spot = frames * rows
+    sems = pltpu.SemaphoreType.DMA
+    return pl.pallas_call(
+        functools.partial(block_kernel, tiles, chunks_one, chunks_two),
+        out_shape=jax.ShapeDtypeStruct(latent.shape[1:], jnp.bfloat16),
+        in_specs=[pl.BlockSpec(memory_space=pltpu.SMEM)] + [vmem] * 6 + [anywhere] * 2,
+        out_specs=vmem,
+        scratch_shapes=[
+            pltpu.VMEM((27, half, channels), jnp.bfloat16),
+            pltpu.VMEM((27, half, channels), jnp.bfloat16),
+            pltpu.VMEM((4, frames, height, own_width, half), jnp.bfloat16),
+            pltpu.VMEM((frames, height, width, half), jnp.float32),
+            pltpu.VMEM((frames + 2, height + 2, width, 3 * half), jnp.bfloat16),
+            pltpu.VMEM((spot * width, half), jnp.bfloat16),
+            pltpu.VMEM((spot * width, half), jnp.bfloat16),
+            pltpu.VMEM((spot * width, half), jnp.float32),
+            pltpu.VMEM((frames, height, width, half), jnp.bfloat16),
+            pltpu.VMEM((spot * width // 2, channels), jnp.bfloat16),
+            pltpu.VMEM((spot * width // 2, channels), jnp.bfloat16),
+            pltpu.VMEM((spot * width // 2, channels), jnp.float32),
+            pltpu.VMEM((frames, rows, own_width, channels), jnp.float32),
+            pltpu.VMEM((frames, rows, own_width, channels), jnp.float32),
+            pltpu.VMEM((OVMAX, height, own_width, channels), jnp.bfloat16),
+            sems((2,)),
+            sems((2,)),
+            sems((2,)),
+            sems((3,)),
+            sems((3,)),
+            sems((len(chunks_one),)),
+            sems((len(chunks_one),)),
+            sems((len(chunks_one),)),
+            sems((len(chunks_one),)),
+            sems((len(chunks_two),)),
+            sems((len(chunks_two),)),
+            sems((len(chunks_two),)),
+            sems((len(chunks_two),)),
+            sems,
+            sems,
+        ],
+        compiler_params=pltpu.CompilerParams(
+            collective_id=0, has_side_effects=True, vmem_limit_bytes=60 * 2**20
+        ),
+    )(
+        intersections,
+        latent[0],
+        gain_one[None],
+        shift_one[None],
+        gain_two[None],
+        shift_two[None],
+        bias[None],
+        weight_one.reshape(27, shard, channels),
+        weight_two.reshape(27, shard, channels),
+    )[None]
+
+
+def program(tiles, cols, *args):
+    _, frames, height, own_width, channels = args[0].shape
+    fits = (
+        cols == 4
+        and channels == 2 * LANES
+        and own_width == 4
+        and height % 2 == 0
+        and frames >= 2 * OVMAX
+    )
+    return fused(tiles, *args) if fits else shards(*args)
+
+
 def solution(mesh):
     in_specs = (
         P("tile", None, None, "col", None),
@@ -129,4 +518,5 @@
         P(),
     )
     out_specs = P("tile", None, None, "col", None)
-    return jax.shard_map(shards, mesh=mesh, in_specs=in_specs, out_specs=out_specs, check_vma=False)
+    return jax.shard_map(
+        functools.partial(program, mesh.shape["tile"], mesh.shape["col"]), mesh=mesh, in_specs=in_specs, out_specs=out_specs, check_vma=False)

time: 123 us -> 27.3 us (0.22)
  local copies, waits for them, and re-layouts: 38 us -> 1.61 us
  blocking collectives: 31.1 us -> 0 us
  Pallas kernels: 0 us -> 24.8 us
  matrix products: 22.3 us -> 0 us
  between operations: 15.1 us -> 0.66 us
  other arithmetic: 6.67 us -> 0 us
  starting transfers between devices: 6.25 us -> 0 us
  waiting for transfers between devices: 2.6 us -> 0 us
    reshape x59 -> x0, local copies, waits for them, and re-layouts: 32.1 us -> none  [the longest x54 31.7 us: conv_taps(): window.reshape(-1, channels)]
    psum x4 -> x0, blocking collectives: 31.1 us -> none  [the longest x2 19 us: norm_silu(): group_mean = lax.psum(chan_sums, 'col') / members]
    pallas_call x0 -> x1, Pallas kernels: none -> 24.8 us  [fused(): pl.pallas_call(functools.partial(block_kernel, tiles, chunks_one, chunks_...]
    dot_general x54 -> x0, matrix products: 22.3 us -> none  [conv_taps(): jnp.dot(window.reshape(-1, channels), kernel[tap_t, tap_h, tap_w], prefer...]
    ppermute x3 -> x0, starting transfers between devices: 6.21 us -> none  [the longest x1 3.63 us: shifted(): return lax.ppermute(block, axis, route)]
    slice x7 -> x0, local copies, waits for them, and re-layouts: 4.46 us -> none  [the longest x4 4.31 us: conv_taps(): padded[tap_t:tap_t + frames, tap_h:tap_h + height, tap_w:tap_w + out_width]]
    reduce_sum x8 -> x0, other arithmetic: 2.8 us -> none  [group_total(): jnp.sum(values, axis=(0, 1, 2)).reshape(GROUPS, per_group).sum(axis=1)]
    ppermute x3 -> x0, waiting for transfers between devices: 1.83 us -> none  [the longest x1 1.51 us: shifted(): return lax.ppermute(block, axis, route)]
  transfers between devices with their start and end apart: 5 -> 0, of which waited for: 2 -> 0; matrix products, arithmetic and copies ran while one was open for 45% -> 0% of each run, Pallas kernels for 0% -> 0%
where the time goes in v1:
time: 27.3 us; the launch traced here: 27.1 us
  Pallas kernels  24.8 us (91%)
  local copies, waits for them, and re-layouts  1.61 us (6%)
  between operations  0.66 us (2%)
    pallas_call x1, Pallas kernels, fused(): pl.pallas_call(functools.partial(block_kernel, tiles, chunks_one, chunks_...  24.8 us
    unnamed x1, local copies, waits for them, and re-layouts  1.61 us

profile of v1, /device:TPU:0, one launch (start us, length us, event | category | flops | bytes accessed | tf_op | source)
XLA Modules:
  0.0 27.1 jit_solution(16602401694168184075)
XLA Ops:
  0.7 24.8 %shard_map.91 = bf16[17,4,4,256]{3,2,1,0:T(4,128)(2,1)} custom-call(s32[1]{0:T(128)S(6)} %copy.11.inter, bf16[17,4,4,256]{3,2,1,0:T(4,128)(2,1)} %bitcast.12, f32[1,256]{1,0:T(1,128)} %bitcast.13, f32[1,256]{1,0:T(1,128)} %bitcast.14, f32[1,256]{1,0:T(1,128)} %bitcast.15, f32[1,256]{1,0:T(1,128)} %bitcast.16, f32[1,256]{1,0:T(1,128)} %bitcast.17, ...), custom_call_target="tpu_custom_call" | custom-call | tf_op jit(solution)/shard_map/pallas_call | solution.py:443
  25.5 1.6 %copy.12 = bf16[1,17,4,4,256]{4,3,2,1,0:T(4,128)(2,1)} copy(bf16[1,17,4,4,256]{4,3,2,1,0:T(4,128)(2,1)} %bitcast.11) | data formatting | bytes 278528

commit v2 on v1

--- a/solution.py
+++ b/solution.py
@@ -136,9 +136,8 @@
     return row
 
 
-def norm_into(lines, taps, gain, shift, per_group):
-    frames = taps.shape[0] - 2
-    height, width = taps.shape[1] - 2, taps.shape[2]
+def norm_into(frames, lines, store, gain, shift, per_group):
+    height, width, _ = lines(0).shape
     members = frames * height * width * per_group
 
     def total(f):
@@ -161,10 +160,7 @@
         a = v / (1.0 + jnp.exp(-v))
         left = jnp.where(where == 0, 0.0, pltpu.roll(a, 1, 1))
         right = jnp.where(where == width - 1, 0.0, pltpu.roll(a, width - 1, 1))
-        place = (t + 2, pl.ds(1, height))
-        taps[place + (slice(None), pl.ds(0, LANES))] = left.astype(jnp.bfloat16)
-        taps[place + (slice(None), pl.ds(LANES, LANES))] = a.astype(jnp.bfloat16)
-        taps[place + (slice(None), pl.ds(2 * LANES, LANES))] = right.astype(jnp.bfloat16)
+        store(t, (left, a, right))
 
 
 def conv_part(taps, weight, first, count, row, rows):
@@ -179,25 +175,37 @@
     return jnp.dot(lhs, rhs, preferred_element_type=jnp.float32)
 
 
+def conv_packed(taps, weight, first, count):
+    rows, depth = taps.shape[1], taps.shape[2]
+    pieces = [taps[pl.ds(first + dt, count)].reshape(count * rows, depth) for dt in range(3)]
+    lhs = jnp.concatenate(pieces, axis=1)
+    rhs = weight[...].reshape(3 * depth, weight.shape[2])
+    return jnp.dot(lhs, rhs, preferred_element_type=jnp.float32)
+
+
 def block_kernel(
     tiles,
     chunks_one,
     chunks_two,
-    inter,
-    lat,
-    gain_one,
-    shift_one,
-    gain_two,
-    shift_two,
-    bias,
+    inter_hbm,
+    lat_hbm,
+    gain_one_hbm,
+    shift_one_hbm,
+    gain_two_hbm,
+    shift_two_hbm,
+    bias_hbm,
     w_one,
     w_two,
     out,
+    inter,
+    lat,
+    small,
     wb_one,
     wb_two,
     got,
     full,
     taps,
+    packed,
     part_out,
     part_in,
     keep_one,
@@ -205,9 +213,8 @@
     mix_out,
     mix_in,
     keep_two,
-    give,
-    take,
     tail_in,
+    in_sem,
     w_local,
     w_send,
     w_recv,
@@ -219,8 +226,6 @@
     h_recv,
     m_send,
     m_recv,
-    g_send,
-    g_recv,
     t_send,
     t_recv,
 ):
@@ -246,6 +251,32 @@
             device_id_type=MESH,
         )
 
+    barrier = pltpu.get_barrier_semaphore()
+    for col in (partner, twin):
+        pl.semaphore_signal(
+            barrier, inc=1, device_id={"tile": tile, "col": col}, device_id_type=MESH
+        )
+
+    @pl.when(tile > 0)
+    def _():
+        pl.semaphore_signal(
+            barrier, inc=1, device_id={"tile": tile - 1, "col": me}, device_id_type=MESH
+        )
+
+    @pl.when(tile < tiles - 1)
+    def _():
+        pl.semaphore_signal(
+            barrier, inc=1, device_id={"tile": tile + 1, "col": me}, device_id_type=MESH
+        )
+
+    lat_copy = pltpu.make_async_copy(lat_hbm, lat, in_sem.at[0])
+    lat_copy.start()
+    vectors = (gain_one_hbm, shift_one_hbm, gain_two_hbm, shift_two_hbm, bias_hbm)
+    loads = [pltpu.make_async_copy(inter_hbm, inter, in_sem.at[1])]
+    for k, vector in enumerate(vectors):
+        loads.append(pltpu.make_async_copy(vector, small.at[k], in_sem.at[2 + k]))
+    for copy in loads:
+        copy.start()
     mine_rows = pl.ds(pl.multiple_of(core * shard, shard), shard)
     w_copies = []
     for k, (w, wb) in enumerate(((w_one, wb_one), (w_two, wb_two))):
@@ -253,65 +284,73 @@
         copy.start()
         w_copies.append(copy)
 
-    barrier = pltpu.get_barrier_semaphore()
-    for col in (partner, twin):
-        pl.semaphore_signal(
-            barrier, inc=1, device_id={"tile": tile, "col": col}, device_id_type=MESH
-        )
-
-    @pl.when(tile > 0)
-    def _():
-        pl.semaphore_signal(
-            barrier, inc=1, device_id={"tile": tile - 1, "col": me}, device_id_type=MESH
-        )
-
-    @pl.when(tile < tiles - 1)
-    def _():
-        pl.semaphore_signal(
-            barrier, inc=1, device_id={"tile": tile + 1, "col": me}, device_id_type=MESH
-        )
-
+    first_chip = chip == 0
+    first_core = core == 0
+    here = pl.ds(pl.multiple_of(chip * half, half), half)
+    there = pl.ds(pl.multiple_of((1 - chip) * half, half), half)
+    to_twin = remote(lat.at[:, :, :, there], got.at[me], l_send.at[0], l_recv.at[0], twin)
+    to_partner = remote(lat.at[:, :, :, here], got.at[me], l_send.at[1], l_recv.at[1], partner)
+    forward = remote(got.at[twin], got.at[twin], l_send.at[2], l_recv.at[2], partner)
+    w_sends = [
+        remote(w, wb.at[:, mine_rows, :], w_send.at[k], w_recv.at[k], partner)
+        for k, (w, wb) in enumerate(((w_one, wb_one), (w_two, wb_two)))
+    ]
+
+    lat_copy.wait()
     pl.semaphore_wait(
         barrier, 2 + jnp.where(tile > 0, 1, 0) + jnp.where(tile < tiles - 1, 1, 0)
     )
-
-    here = pl.ds(pl.multiple_of(chip * half, half), half)
-    there = pl.ds(pl.multiple_of((1 - chip) * half, half), half)
-    to_twin = remote(lat.at[:, :, :, there], got.at[me], l_send.at[0], l_recv.at[0], twin)
     to_twin.start()
-    to_partner = remote(lat.at[:, :, :, here], got.at[me], l_send.at[1], l_recv.at[1], partner)
     to_partner.start()
-    w_sends = []
-    for k, (w, wb) in enumerate(((w_one, wb_one), (w_two, wb_two))):
-        copy = remote(w, wb.at[:, mine_rows, :], w_send.at[k], w_recv.at[k], partner)
-        copy.start()
-        w_sends.append(copy)
-
+    w_sends[0].start()
+
+    got[me] = jnp.where(first_chip, lat[:, :, :, :half], lat[:, :, :, half:])
     taps[0:2] = jnp.zeros((2,) + taps.shape[1:], taps.dtype)
     edge = jnp.zeros((frames,) + taps.shape[2:], taps.dtype)
     taps[2:, 0] = edge
     taps[2:, height + 1] = edge
-
-    first_chip = chip == 0
-    first_core = core == 0
-
-    def chosen(ref):
-        return jnp.where(first_chip, ref[:, :half], ref[:, half:])
-
-    got[me] = jnp.where(first_chip, lat[:, :, :, :half], lat[:, :, :, half:])
+    packed[0:2] = jnp.zeros((2,) + packed.shape[1:], packed.dtype)
+
+    for copy in loads:
+        copy.wait()
+
+    def chosen(k):
+        return jnp.where(first_chip, small[k][:, :half], small[k][:, half:])
+
+    def store_taps(t, three):
+        for k, value in enumerate(three):
+            place = (t + 2, pl.ds(1, height), slice(None), pl.ds(k * LANES, LANES))
+            taps[place] = value.astype(jnp.bfloat16)
+
+    cols = 2 * own_width
+    sub = lax.broadcasted_iota(jnp.int32, (height, cols, LANES), 1)
+
+    def store_packed(t, three):
+        zero = jnp.zeros((1, cols, LANES), jnp.float32)
+        for k, value in enumerate(three):
+            lo, hi = value[:, :cols], value[:, cols:]
+            low = jnp.where(first_core, lo, pltpu.roll(lo, own_width, 1))
+            high = jnp.where(first_core, pltpu.roll(hi, own_width, 1), hi)
+            line = jnp.where(sub < own_width, low, high)
+            moved = (
+                jnp.concatenate([zero, line[:-1]], axis=0),
+                line,
+                jnp.concatenate([line[1:], zero], axis=0),
+            )
+            for dh, lines in enumerate(moved):
+                value = lines.reshape(height * cols, LANES).astype(jnp.bfloat16)
+                packed[t + 2, :, pl.ds((dh * 3 + k) * LANES, LANES)] = value
 
     to_twin.wait_recv()
-    forward = remote(got.at[twin], got.at[twin], l_send.at[2], l_recv.at[2], partner)
     forward.start()
+    w_sends[1].start()
     to_partner.wait_recv()
     forward.wait_recv()
     for i in range(4):
         full[:, :, i * own_width : (i + 1) * own_width, :] = got[i].astype(jnp.float32)
 
     per_group = channels // GROUPS
-    norm_into(
-        lambda t: full[t], taps, chosen(gain_one), chosen(shift_one), per_group
-    )
+    norm_into(frames, lambda t: full[t], store_taps, chosen(0), chosen(1), per_group)
 
     w_copies[0].wait()
     w_sends[0].wait()
@@ -341,31 +380,29 @@
         copy.wait_recv()
 
     norm_into(
-        lambda t: hid[t].astype(jnp.float32), taps, chosen(gain_two), chosen(shift_two), per_group
+        frames,
+        lambda t: hid[t].astype(jnp.float32),
+        store_packed,
+        chosen(2),
+        chosen(3),
+        per_group,
     )
 
     w_copies[1].wait()
     w_sends[1].wait()
-    cols = 2 * own_width
+    offset = small[4][None, None]
     sends_two = []
     for k, (first, count) in enumerate(chunks_two):
-        acc = conv_part(taps, wb_two, first, count, row, rows)
-        acc = acc.reshape(count * rows, width, channels)
-        lo, hi = acc[:, :cols], acc[:, cols:]
-        span = pl.ds(first * rows * cols, count * rows * cols)
-        away = jnp.where(first_chip, hi, lo).reshape(count * rows * cols, channels)
-        mix_out[span] = away.astype(jnp.bfloat16)
-        copy = remote(mix_out.at[span], mix_in.at[span], m_send.at[k], m_recv.at[k], twin)
+        acc = conv_packed(packed, wb_two, first, count)
+        acc = acc.reshape(count, height, cols, channels)
+        lo, hi = acc[:, :, :own_width], acc[:, :, own_width:]
+        times = pl.ds(first, count)
+        mix_out[times] = jnp.where(first_chip, hi, lo).astype(jnp.bfloat16)
+        copy = remote(mix_out.at[times], mix_in.at[times], m_send.at[k], m_recv.at[k], twin)
         copy.start()
-        keep_two[span] = jnp.where(first_chip, lo, hi).reshape(count * rows * cols, channels)
-        sends_two.append((copy, span, first, count))
-
-    other_row = (1 - core) * rows
-    offset = bias[...][None, None]
-
-    def finish(place, values):
-        own = lat[place].astype(jnp.float32)
-        out[place] = (own + (values + offset)).astype(jnp.bfloat16)
+        own = jnp.where(first_chip, lo, hi)
+        keep_two[times] = lat[times].astype(jnp.float32) + (own + offset)
+        sends_two.append((copy, times))
 
     overlap = OVMAX
     next_tile = jnp.minimum(tile + 1, tiles - 1)
@@ -377,22 +414,10 @@
         device_id={"tile": next_tile, "col": me},
         device_id_type=MESH,
     )
-    gives = []
-    for k, (copy, span, first, count) in enumerate(sends_two):
+    for k, (copy, times) in enumerate(sends_two):
         copy.wait_recv()
-        value = keep_two[span] + mix_in[span].astype(jnp.float32)
-        value = value.reshape(count * rows, cols, channels)
-        lo, hi = value[:, :own_width], value[:, own_width:]
-        times = pl.ds(first, count)
-        theirs = jnp.where(first_core, hi, lo)
-        give[times] = theirs.reshape(count, rows, own_width, channels)
-        swap = remote(give.at[times], take.at[times], g_send.at[k], g_recv.at[k], partner)
-        swap.start()
-        gives.append(swap)
-        ours = jnp.where(first_core, lo, hi).reshape(count, rows, own_width, channels)
-        finish((times, pl.ds(row, rows)), ours)
-        swap.wait_recv()
-        finish((times, pl.ds(other_row, rows)), take[times])
+        value = keep_two[times] + mix_in[times].astype(jnp.float32)
+        out[times] = value.astype(jnp.bfloat16)
         if k == 0:
 
             @pl.when(tile < tiles - 1)
@@ -419,9 +444,9 @@
     to_twin.wait_send()
     to_partner.wait_send()
     forward.wait_send()
-    for copy, _, _, _ in sends + sends_two:
+    for copy, *_ in sends + sends_two:
         copy.wait_send()
-    for copy in back + gives:
+    for copy in back:
         copy.wait_send()
 
     @pl.when(tile < tiles - 1)
@@ -432,35 +457,40 @@
 def fused(tiles, latent, intersections, gain_one, shift_one, weight_one, gain_two, shift_two, weight_two, bias):
     _, frames, height, own_width, channels = latent.shape
     width, half, rows = 4 * own_width, channels // 2, height // 2
-    ahead = (frames + 1) // 2
-    chunks_one = (ahead, frames - ahead)
-    chunks_two = ((frames - OVMAX, OVMAX), (0, frames - OVMAX))
+    early = frames // 4
+    middle = (frames - early) // 2
+    chunks_one = (early, middle, frames - early - middle)
+    rest = frames - OVMAX
+    chunks_two = ((rest, OVMAX), (0, rest // 2), (rest // 2, rest - rest // 2))
     shard = weight_one.shape[3]
-    vmem = pl.BlockSpec(memory_space=pltpu.VMEM)
     anywhere = pl.BlockSpec(memory_space=pl.ANY)
     spot = frames * rows
     sems = pltpu.SemaphoreType.DMA
+    own_block = latent.shape[1:]
     return pl.pallas_call(
         functools.partial(block_kernel, tiles, chunks_one, chunks_two),
-        out_shape=jax.ShapeDtypeStruct(latent.shape[1:], jnp.bfloat16),
-        in_specs=[pl.BlockSpec(memory_space=pltpu.SMEM)] + [vmem] * 6 + [anywhere] * 2,
-        out_specs=vmem,
+        out_shape=pltpu.VMEM(own_block, jnp.bfloat16),
+        in_specs=[pl.BlockSpec(memory_space=pltpu.HBM)] * 9,
+        out_specs=pl.BlockSpec(memory_space=pltpu.VMEM),
         scratch_shapes=[
+            pltpu.SMEM((1,), jnp.int32),
+            pltpu.VMEM(own_block, jnp.bfloat16),
+            pltpu.VMEM((5, 1, channels), jnp.float32),
             pltpu.VMEM((27, half, channels), jnp.bfloat16),
             pltpu.VMEM((27, half, channels), jnp.bfloat16),
             pltpu.VMEM((4, frames, height, own_width, half), jnp.bfloat16),
             pltpu.VMEM((frames, height, width, half), jnp.float32),
             pltpu.VMEM((frames + 2, height + 2, width, 3 * half), jnp.bfloat16),
+            pltpu.VMEM((frames + 2, height * 2 * own_width, 9 * half), jnp.bfloat16),
             pltpu.VMEM((spot * width, half), jnp.bfloat16),
             pltpu.VMEM((spot * width, half), jnp.bfloat16),
             pltpu.VMEM((spot * width, half), jnp.float32),
             pltpu.VMEM((frames, height, width, half), jnp.bfloat16),
-            pltpu.VMEM((spot * width // 2, channels), jnp.bfloat16),
-            pltpu.VMEM((spot * width // 2, channels), jnp.bfloat16),
-            pltpu.VMEM((spot * width // 2, channels), jnp.float32),
-            pltpu.VMEM((frames, rows, own_width, channels), jnp.float32),
-            pltpu.VMEM((frames, rows, own_width, channels), jnp.float32),
-            pltpu.VMEM((OVMAX, height, own_width, channels), jnp.bfloat16),
+            pltpu.VMEM(own_block, jnp.bfloat16),
+            pltpu.VMEM(own_block, jnp.bfloat16),
+            pltpu.VMEM(own_block, jnp.float32),
+            pltpu.VMEM((OVMAX,) + own_block[1:], jnp.bfloat16),
+            sems((7,)),
             sems((2,)),
             sems((2,)),
             sems((2,)),
@@ -470,8 +500,6 @@
             sems((len(chunks_one),)),
             sems((len(chunks_one),)),
             sems((len(chunks_one),)),
-            sems((len(chunks_two),)),
-            sems((len(chunks_two),)),
             sems((len(chunks_two),)),
             sems((len(chunks_two),)),
             sems,

time: 27.3 us -> 23.5 us (0.86)
  Pallas kernels: 24.8 us -> 22.1 us
  local copies, waits for them, and re-layouts: 1.61 us -> 0.66 us
    pallas_call x1, Pallas kernels: 24.8 us -> 22.1 us  [fused(): pl.pallas_call(functools.partial(block_kernel, tiles, chunks_one, chunks_...]
    unnamed x1, local copies, waits for them, and re-layouts: 1.61 us -> 0.66 us
where the time goes in v2:
time: 23.5 us; the launch traced here: 23.4 us
  Pallas kernels  22.1 us (94%)
  local copies, waits for them, and re-layouts  0.66 us (3%)
  between operations  0.66 us (3%)
    pallas_call x1, Pallas kernels, fused(): pl.pallas_call(functools.partial(block_kernel, tiles, chunks_one, chunks_...  22.1 us
    unnamed x1, local copies, waits for them, and re-layouts  0.66 us

profile of v2, /device:TPU:0, one launch (start us, length us, event | category | flops | bytes accessed | tf_op | source)
XLA Modules:
  0.0 23.4 jit_solution(4923170889566313161)
XLA Ops:
  0.7 22.1 %shard_map.91 = bf16[17,4,4,256]{3,2,1,0:T(4,128)(2,1)S(1)} custom-call(s32[1]{0:T(128)S(6)} %copy.12.inter_hbm, bf16[17,4,4,256]{3,2,1,0:T(4,128)(2,1)} %bitcast.12, f32[1,256]{1,0:T(1,128)} %bitcast.13, f32[1,256]{1,0:T(1,128)} %bitcast.14, f32[1,256]{1,0:T(1,128)} %bitcast.15, f32[1,256]{1,0:T(1,128)} %bitcast.16, f32[1,256]{1,0:T(1,128)} %bitcast.17, ...), custom_call_target="tpu_custom_call" | custom-call | tf_op jit(solution)/shard_map/pallas_call | solution.py:470
  22.7 0.7 %copy.11 = bf16[1,17,4,4,256]{4,3,2,1,0:T(4,128)(2,1)} copy(bf16[1,17,4,4,256]{4,3,2,1,0:T(4,128)(2,1)S(1)} %bitcast.9) | data formatting | bytes 278528

commit v3 on v2

--- a/solution.py
+++ b/solution.py
@@ -136,7 +136,7 @@
     return row
 
 
-def norm_into(frames, lines, store, gain, shift, per_group):
+def norm_of(frames, lines, store, gain, shift, per_group):
     height, width, _ = lines(0).shape
     members = frames * height * width * per_group
 
@@ -155,12 +155,18 @@
 
     scale = lax.rsqrt(total(square) + epsilon)
     where = lax.broadcasted_iota(jnp.int32, (height, width, LANES), 1)
-    for t in range(frames):
-        v = (lines(t) - mean[None]) * scale[None] * gain[None] + shift[None]
-        a = v / (1.0 + jnp.exp(-v))
-        left = jnp.where(where == 0, 0.0, pltpu.roll(a, 1, 1))
-        right = jnp.where(where == width - 1, 0.0, pltpu.roll(a, width - 1, 1))
-        store(t, (left, a, right))
+    factor = scale * gain
+
+    def normalise(times):
+        for t in times:
+            v = (lines(t) - mean[None]) * factor[None] + shift[None]
+            b = 0.5 * v
+            a = b + b * jnp.tanh(b)
+            left = jnp.where(where == 0, 0.0, pltpu.roll(a, 1, 1))
+            right = jnp.where(where == width - 1, 0.0, pltpu.roll(a, width - 1, 1))
+            store(t, (left, a, right))
+
+    return normalise
 
 
 def conv_part(taps, weight, first, count, row, rows):
@@ -263,12 +269,6 @@
             barrier, inc=1, device_id={"tile": tile - 1, "col": me}, device_id_type=MESH
         )
 
-    @pl.when(tile < tiles - 1)
-    def _():
-        pl.semaphore_signal(
-            barrier, inc=1, device_id={"tile": tile + 1, "col": me}, device_id_type=MESH
-        )
-
     lat_copy = pltpu.make_async_copy(lat_hbm, lat, in_sem.at[0])
     lat_copy.start()
     vectors = (gain_one_hbm, shift_one_hbm, gain_two_hbm, shift_two_hbm, bias_hbm)
@@ -297,9 +297,7 @@
     ]
 
     lat_copy.wait()
-    pl.semaphore_wait(
-        barrier, 2 + jnp.where(tile > 0, 1, 0) + jnp.where(tile < tiles - 1, 1, 0)
-    )
+    pl.semaphore_wait(barrier, 2 + jnp.where(tile < tiles - 1, 1, 0))
     to_twin.start()
     to_partner.start()
     w_sends[0].start()
@@ -350,14 +348,16 @@
         full[:, :, i * own_width : (i + 1) * own_width, :] = got[i].astype(jnp.float32)
 
     per_group = channels // GROUPS
-    norm_into(frames, lambda t: full[t], store_taps, chosen(0), chosen(1), per_group)
-
-    w_copies[0].wait()
-    w_sends[0].wait()
+    normalise = norm_of(frames, lambda t: full[t], store_taps, chosen(0), chosen(1), per_group)
+
     row = core * rows
     sends = []
     start = 0
     for k, count in enumerate(chunks_one):
+        normalise(range(start, start + count))
+        if k == 0:
+            w_copies[0].wait()
+            w_sends[0].wait()
         acc = conv_part(taps, wb_one, start, count, row, rows)
         lo, hi = acc[:, :half], acc[:, half:]
         span = pl.ds(start * rows * width, count * rows * width)
@@ -379,7 +379,7 @@
     for copy in back:
         copy.wait_recv()
 
-    norm_into(
+    normalise = norm_of(
         frames,
         lambda t: hid[t].astype(jnp.float32),
         store_packed,
@@ -388,11 +388,16 @@
         per_group,
     )
 
-    w_copies[1].wait()
-    w_sends[1].wait()
+    done = set()
     offset = small[4][None, None]
     sends_two = []
     for k, (first, count) in enumerate(chunks_two):
+        needed = [t for t in range(max(first - 2, 0), first + count) if t not in done]
+        normalise(needed)
+        done.update(needed)
+        if k == 0:
+            w_copies[1].wait()
+            w_sends[1].wait()
         acc = conv_packed(packed, wb_two, first, count)
         acc = acc.reshape(count, height, cols, channels)
         lo, hi = acc[:, :, :own_width], acc[:, :, own_width:]

time: 23.5 us -> 22.9 us (0.974)
  Pallas kernels: 22.1 us -> 21.5 us
    pallas_call x1, Pallas kernels: 22.1 us -> 21.5 us  [fused(): pl.pallas_call(functools.partial(block_kernel, tiles, chunks_one, chunks_...]
where the time goes in v3:
time: 22.9 us; the launch traced here: 22.8 us
  Pallas kernels  21.5 us (94%)
  local copies, waits for them, and re-layouts  0.66 us (3%)
  between operations  0.66 us (3%)
    pallas_call x1, Pallas kernels, fused(): pl.pallas_call(functools.partial(block_kernel, tiles, chunks_one, chunks_...  21.5 us
    unnamed x1, local copies, waits for them, and re-layouts  0.66 us

profile of v3, /device:TPU:0, one launch (start us, length us, event | category | flops | bytes accessed | tf_op | source)
XLA Modules:
  0.0 22.8 jit_solution(2941068774708747422)
XLA Ops:
  0.7 21.5 %shard_map.91 = bf16[17,4,4,256]{3,2,1,0:T(4,128)(2,1)S(1)} custom-call(s32[1]{0:T(128)S(6)} %copy.12.inter_hbm, bf16[17,4,4,256]{3,2,1,0:T(4,128)(2,1)} %bitcast.12, f32[1,256]{1,0:T(1,128)} %bitcast.13, f32[1,256]{1,0:T(1,128)} %bitcast.14, f32[1,256]{1,0:T(1,128)} %bitcast.15, f32[1,256]{1,0:T(1,128)} %bitcast.16, f32[1,256]{1,0:T(1,128)} %bitcast.17, ...), custom_call_target="tpu_custom_call" | custom-call | tf_op jit(solution)/shard_map/pallas_call | solution.py:475
  22.1 0.7 %copy.11 = bf16[1,17,4,4,256]{4,3,2,1,0:T(4,128)(2,1)} copy(bf16[1,17,4,4,256]{4,3,2,1,0:T(4,128)(2,1)S(1)} %bitcast.9) | data formatting | bytes 278528

commit v4 on v3

--- a/solution.py
+++ b/solution.py
@@ -339,16 +339,21 @@
                 value = lines.reshape(height * cols, LANES).astype(jnp.bfloat16)
                 packed[t + 2, :, pl.ds((dh * 3 + k) * LANES, LANES)] = value
 
+    def widen(side):
+        for k in range(2):
+            span = slice(k * own_width, (k + 1) * own_width)
+            full[:, :, side, span, :] = got[2 * side + k].astype(jnp.float32)
+
+    to_partner.wait_recv()
+    widen(chip)
     to_twin.wait_recv()
     forward.start()
     w_sends[1].start()
-    to_partner.wait_recv()
     forward.wait_recv()
-    for i in range(4):
-        full[:, :, i * own_width : (i + 1) * own_width, :] = got[i].astype(jnp.float32)
+    widen(1 - chip)
 
     per_group = channels // GROUPS
-    normalise = norm_of(frames, lambda t: full[t], store_taps, chosen(0), chosen(1), per_group)
+    normalise = norm_of(frames, lambda t: full[t].reshape(height, width, half), store_taps, chosen(0), chosen(1), per_group)
 
     row = core * rows
     sends = []
@@ -484,7 +489,7 @@
             pltpu.VMEM((27, half, channels), jnp.bfloat16),
             pltpu.VMEM((27, half, channels), jnp.bfloat16),
             pltpu.VMEM((4, frames, height, own_width, half), jnp.bfloat16),
-            pltpu.VMEM((frames, height, width, half), jnp.float32),
+            pltpu.VMEM((frames, height, 2, width // 2, half), jnp.float32),
             pltpu.VMEM((frames + 2, height + 2, width, 3 * half), jnp.bfloat16),
             pltpu.VMEM((frames + 2, height * 2 * own_width, 9 * half), jnp.bfloat16),
             pltpu.VMEM((spot * width, half), jnp.bfloat16),

time: 22.9 us -> 22.9 us (level)
  no operation moved by 1% of the time
where the time goes in v4:
time: 22.9 us; the launch traced here: 22.8 us
  Pallas kernels  21.5 us (94%)
  local copies, waits for them, and re-layouts  0.66 us (3%)
  between operations  0.66 us (3%)
    pallas_call x1, Pallas kernels, fused(): pl.pallas_call(functools.partial(block_kernel, tiles, chunks_one, chunks_...  21.5 us
    unnamed x1, local copies, waits for them, and re-layouts  0.66 us

profile of v4, /device:TPU:0, one launch (start us, length us, event | category | flops | bytes accessed | tf_op | source)
XLA Modules:
  0.0 22.8 jit_solution(10233379670451290876)
XLA Ops:
  0.7 21.5 %shard_map.91 = bf16[17,4,4,256]{3,2,1,0:T(4,128)(2,1)S(1)} custom-call(s32[1]{0:T(128)S(6)} %copy.12.inter_hbm, bf16[17,4,4,256]{3,2,1,0:T(4,128)(2,1)} %bitcast.12, f32[1,256]{1,0:T(1,128)} %bitcast.13, f32[1,256]{1,0:T(1,128)} %bitcast.14, f32[1,256]{1,0:T(1,128)} %bitcast.15, f32[1,256]{1,0:T(1,128)} %bitcast.16, f32[1,256]{1,0:T(1,128)} %bitcast.17, ...), custom_call_target="tpu_custom_call" | custom-call | tf_op jit(solution)/shard_map/pallas_call | solution.py:480
  22.1 0.7 %copy.11 = bf16[1,17,4,4,256]{4,3,2,1,0:T(4,128)(2,1)} copy(bf16[1,17,4,4,256]{4,3,2,1,0:T(4,128)(2,1)S(1)} %bitcast.9) | data formatting | bytes 278528
